TPU v7x, 128 devices: a whole 4x4x4 slice. The times are simulated.
128 devices in a mesh: row: 16 (over x_hi, y, core), col: 8 (over z, x_lo).
Axes of the slice: x: 4 (x_hi: 2, x_lo: 2; x = x_hi * 2 + x_lo), y: 4, z: 4, core: 2. Of those that a mesh axis runs over, the one named last changes fastest.
Arguments:
- constraint_tiles: float32 [1536, 8, 128, 128], P('row', 'col'), may hold values from -0.25 to 0.25
- constraint_rows: int32 [1536, 8], P('row', 'col'), may hold values from 0 to 191
- constraint_cols: int32 [1536, 8], P('row', 'col'), may hold values from 0 to 255
- factor_tiles: float32 [768, 8, 128, 128], P('row', 'col'), may hold values from -0.21875 to 0.21875
- factor_rows: int32 [768, 8], P('row', 'col'), may hold values from 0 to 63
- factor_cols: int32 [768, 8], P('row', 'col'), may hold values from 0 to 255
- diag_cost: float32 [2048, 128], P('col'), may hold values from 0.1 to 1
- linear_cost: float32 [2048, 128], P('col'), may hold values from -6 to 6
- lower_bound: float32 [3072, 128], P('row'), may hold values from -1.5 to -0.2
- upper_bound: float32 [3072, 128], P('row'), may hold values from 0.2 to 1.5
- primal_start: float32 [2048, 128], P('col'), may hold values from -6 to 6
- slack_start: float32 [3072, 128], P('row'), may hold values from -6 to 6
- dual_start: float32 [3072, 128], P('row'), may hold values from -6 to 6
- penalty: float32 [], replicated, may hold values from 3 to 6
Outputs:
- primal_next: float32 [2048, 128], P('col')
- slack_next: float32 [3072, 128], P('row')
- dual_next: float32 [3072, 128], P('row')
- primal_res: float32 [], replicated
- dual_res: float32 [], replicated
All inputs are finite; a program needn't handle non-finite values.
Results may differ from a plain program's by a relative error of at most 0.0003.
Values sent between devices are 32-bit elements; how exact they have to be, the bound alone decides.
A program may use at most 128 MiB of HBM per device.

v0:
```python
import functools

import jax
import jax.numpy as jnp
from jax import lax
from jax.sharding import Mesh
from jax.sharding import PartitionSpec as P

YG = 64
CG = 6
ROW = ("row_0", "row_1", "row_2")
COL = ("col_0", "col_1")
ROW_COL = ("row_0", "row_1", "row_2", "col_0", "col_1")


SIGMA = 1e-06
RELAX = 1.6
HIGH = lax.Precision.HIGHEST


def sent_to_all(shard, axis):
    copies = jnp.broadcast_to(shard, (lax.axis_size(axis), *shard.shape))
    return lax.all_to_all(copies, axis, split_axis=0, concat_axis=0, tiled=True)


def over_copies(shard, axis):
    return sent_to_all(shard, axis).sum(axis=0)


def over_axes(shard, axes):
    return functools.reduce(lax.pmax, axes, shard)


def add_blocks(parts, index, count):
    onehot = (jnp.arange(count, dtype=jnp.int32)[:, None] == index[None, :]).astype(jnp.float32)
    return jnp.dot(onehot, parts, precision=HIGH)


def forward_tiles(tiles, rows, cols, vec, count):
    prod = jnp.einsum("kij,kj->ki", tiles, jnp.take(vec, cols, axis=0), precision=HIGH)
    return add_blocks(prod, rows, count)


def backward_tiles(tiles, rows, cols, vec, count):
    prod = jnp.einsum("kij,ki->kj", tiles, jnp.take(vec, rows, axis=0), precision=HIGH)
    return add_blocks(prod, cols, count)


def reduce_rows(parts):
    return jax.tree.map(lambda part: over_copies(part, ROW), parts)


def inner_sums(values):
    return jax.tree.map(lambda part: over_copies(part, COL), values)


def local(
    constraint_tiles,
    constraint_rows,
    constraint_cols,
    factor_tiles,
    factor_rows,
    factor_cols,
    diag_cost,
    linear_cost,
    lower_bound,
    upper_bound,
    primal_start,
    slack_start,
    dual_start,
    penalty,
):
    width = constraint_tiles.shape[2]
    ctiles = constraint_tiles.reshape(-1, width, width)
    ftiles = factor_tiles.reshape(-1, width, width)
    crow = constraint_rows.reshape(-1)
    ccol = constraint_cols.reshape(-1)
    frow = factor_rows.reshape(-1)
    fcol = factor_cols.reshape(-1)
    xcount = primal_start.shape[0]
    ycount = slack_start.shape[0]
    gcount = YG

    def products(full, with_factor):
        avec = forward_tiles(ctiles, crow, ccol, full, ycount)
        parts = (avec, forward_tiles(ftiles, frow, fcol, full, gcount)) if with_factor else (avec,)
        return jax.tree.map(lambda part: over_copies(part, COL), parts)

    def transposed(avec, gvec):
        return backward_tiles(ctiles, crow, ccol, avec, xcount) + backward_tiles(
            ftiles, frow, fcol, gvec, xcount
        )

    shifted = diag_cost + SIGMA

    def apply_k(share):
        avec, gvec = products(share, True)
        summed = reduce_rows((transposed(penalty * avec, gvec),))
        return shifted * share + summed[0]

    avec, gvec = products(primal_start, True)
    kx_part = transposed(penalty * avec, gvec)
    rhs_part = backward_tiles(ctiles, crow, ccol, penalty * slack_start - dual_start, xcount)
    sq_part = penalty * add_blocks(jnp.sum(ctiles * ctiles, axis=1), ccol, xcount) + add_blocks(
        jnp.sum(ftiles * ftiles, axis=1), fcol, xcount
    )
    kx_sum, rhs_sum, sq_sum = reduce_rows((kx_part, rhs_part, sq_part))
    precond = shifted + sq_sum
    rhs = SIGMA * primal_start - linear_cost + rhs_sum
    solution = primal_start
    resid = rhs - (shifted * primal_start + kx_sum)
    scaled = resid / precond
    image = apply_k(scaled)
    gamma, delta = inner_sums((jnp.sum(resid * scaled), jnp.sum(image * scaled)))
    alpha = gamma / delta
    direction = scaled
    along = image
    for step in range(CG):
        solution = solution + alpha * direction
        resid = resid - alpha * along
        if step + 1 < CG:
            scaled = resid / precond
            image = apply_k(scaled)
            gamma_new, delta = inner_sums((jnp.sum(resid * scaled), jnp.sum(image * scaled)))
            ratio = gamma_new / gamma
            alpha = gamma_new / (delta - ratio * gamma_new / alpha)
            direction = scaled + ratio * direction
            along = image + ratio * along
            gamma = gamma_new
    tilde_z = products(solution, False)[0]
    primal_next = RELAX * solution + (1.0 - RELAX) * primal_start
    relaxed = RELAX * tilde_z + (1.0 - RELAX) * slack_start
    slack_next = jnp.minimum(jnp.maximum(relaxed + dual_start / penalty, lower_bound), upper_bound)
    dual_next = dual_start + penalty * (relaxed - slack_next)
    image_next, gnext = products(primal_next, True)
    primal_local = jnp.max(jnp.abs(image_next - slack_next))
    dual_sum = reduce_rows((transposed(dual_next, gnext),))[0]
    dvec = diag_cost * primal_next + dual_sum + linear_cost
    dual_local = jnp.max(jnp.abs(dvec))
    primal_res, dual_res = (over_axes(primal_local, ROW_COL), over_axes(dual_local, ROW_COL))
    return (primal_next, slack_next, dual_next, primal_res, dual_res)


def solution(mesh):
    torus = Mesh(mesh.devices.reshape(2, 4, 2, 4, 2), ("row_0", "row_1", "row_2", "col_0", "col_1"))
    return jax.shard_map(
        local,
        mesh=torus,
        in_specs=(
            P(ROW, COL, None, None),
            P(ROW, COL),
            P(ROW, COL),
            P(ROW, COL, None, None),
            P(ROW, COL),
            P(ROW, COL),
            P(COL, None),
            P(COL, None),
            P(ROW, None),
            P(ROW, None),
            P(COL, None),
            P(ROW, None),
            P(ROW, None),
            P(),
        ),
        out_specs=(P(COL, None), P(ROW, None), P(ROW, None), P(), P()),
        check_vma=False,
    )
```

profile of v0, /device:TPU:1, one launch (start us, length us, event | category | flops | bytes accessed | tf_op | source)
XLA Modules:
  0.0 1039.8 jit_solution(4876834185500846713)
XLA Ops:
  3.6 6.9 fusion.67
  11.3 6.8 all-to-all-start.2
  19.5 13.0 %fusion.32 = f32[96,1,128]{2,1,0:T(1,128)} fusion(f32[96,128,1]{1,2,0:T(1,128)S(1)} %bitcast.339, f32[96,1,128,128]{3,2,1,0:T(8,128)} %param.22), kind=kOutput, calls=%fused_computation.67 | convolution fusion | flops 18874368 | bytes 6389760 | tf_op jit(solution)/shard_map/kij,kj->ki/dot_general | solution.py:40
  45.8 9.3 all-to-all-done.1
  57.5 9.4 all-to-all-start.4
  72.4 7.3 fusion.34
  80.0 15.2 %all-to-all-done.4 = f32[16,256,128]{2,1,0:T(8,128)} async-done(((f32[16,256,128]{2,1,0:T(8,128)}), f32[16,256,128]{2,1,0:T(8,128)}, u32[]{:S(2)}, u32[]{:S(2)}) %all-to-all-start.4) | async-done | bytes 2097184 | tf_op jit(solution)/shard_map/all_to_all | solution.py:23
  96.7 7.0 all-to-all-start
  108.1 7.3 fusion.30
  115.9 16.3 %all-to-all-done = f32[16,256,128]{2,1,0:T(8,128)} async-done(((f32[16,256,128]{2,1,0:T(8,128)}), f32[16,256,128]{2,1,0:T(8,128)}, u32[]{:S(2)}, u32[]{:S(2)}) %all-to-all-start) | async-done | bytes 2097184 | tf_op jit(solution)/shard_map/all_to_all | solution.py:23
  133.7 7.3 all-to-all-start.3
  145.7 23.5 %all-to-all-done.3 = f32[16,256,128]{2,1,0:T(8,128)} async-done(((f32[16,256,128]{2,1,0:T(8,128)}), f32[16,256,128]{2,1,0:T(8,128)}, u32[]{:S(2)}, u32[]{:S(2)}) %all-to-all-start.3) | async-done | bytes 2097184 | tf_op jit(solution)/shard_map/all_to_all | solution.py:23
  185.0 11.8 %fusion.28 = f32[96,1,128]{2,1,0:T(1,128)S(1)} fusion(f32[96,128,1]{1,2,0:T(1,128)S(1)} %bitcast.332, f32[96,1,128,128]{3,2,1,0:T(8,128)} %param.22), kind=kOutput, calls=%fused_computation.62 | convolution fusion | flops 18874368 | bytes 6389760 | tf_op jit(solution)/shard_map/kij,kj->ki/dot_general | solution.py:40
  198.0 5.5 all-to-all-start.6
  208.6 6.4 all-to-all-done.6
  219.2 7.3 fusion.26
  227.2 37.3 %all_to_all.207 = f32[16,256,128]{2,1,0:T(8,128)} all-to-all(f32[16,256,128]{2,1,0:T(8,128)S(1)} %broadcast_in_dim.197), channel_id=1, replica_groups=mesh['row_0'=2,'row_1'=4,'row_2'=2,'col_0'=4,'col_1'=2] {'row_0','row_1'..., dimensions={0} | all-to-all | bytes 4194304 | tf_op jit(solution)/shard_map/all_to_all | solution.py:23
  269.8 7.4 all_to_all.208
  301.9 11.8 %fusion.24 = f32[96,1,128]{2,1,0:T(1,128)S(1)} fusion(f32[96,128,1]{1,2,0:T(1,128)S(1)} %bitcast.333, f32[96,1,128,128]{3,2,1,0:T(8,128)} %param.22), kind=kOutput, calls=%fused_computation.58 | convolution fusion | flops 18874368 | bytes 6389760 | tf_op jit(solution)/shard_map/kij,kj->ki/dot_general | solution.py:40
  333.5 7.3 fusion.22
  341.4 36.5 %all_to_all.209 = f32[16,256,128]{2,1,0:T(8,128)} all-to-all(f32[16,256,128]{2,1,0:T(8,128)S(1)} %broadcast_in_dim.202), channel_id=1, replica_groups=mesh['row_0'=2,'row_1'=4,'row_2'=2,'col_0'=4,'col_1'=2] {'row_0','row_1'..., dimensions={0} | all-to-all | bytes 4194304 | tf_op jit(solution)/shard_map/all_to_all | solution.py:23
  381.9 8.1 all_to_all.210
  420.1 11.9 %fusion.20 = f32[96,1,128]{2,1,0:T(1,128)S(1)} fusion(f32[96,128,1]{1,2,0:T(1,128)} %bitcast.334, f32[96,1,128,128]{3,2,1,0:T(8,128)} %param.22), kind=kOutput, calls=%fused_computation.54 | convolution fusion | flops 18874368 | bytes 6389760 | tf_op jit(solution)/shard_map/kij,kj->ki/dot_general | solution.py:40
  434.6 5.6 all-to-all-start.16
  456.2 7.3 fusion.18
  464.1 35.9 %all_to_all.211 = f32[16,256,128]{2,1,0:T(8,128)} all-to-all(f32[16,256,128]{2,1,0:T(8,128)S(1)} %broadcast_in_dim.207), channel_id=1, replica_groups=mesh['row_0'=2,'row_1'=4,'row_2'=2,'col_0'=4,'col_1'=2] {'row_0','row_1'..., dimensions={0} | all-to-all | bytes 4194304 | tf_op jit(solution)/shard_map/all_to_all | solution.py:23
  504.7 7.4 all_to_all.212
  540.3 11.9 %fusion.16 = f32[96,1,128]{2,1,0:T(1,128)S(1)} fusion(f32[96,128,1]{1,2,0:T(1,128)} %bitcast.335, f32[96,1,128,128]{3,2,1,0:T(8,128)} %param.22), kind=kOutput, calls=%fused_computation.50 | convolution fusion | flops 18874368 | bytes 6389760 | tf_op jit(solution)/shard_map/kij,kj->ki/dot_general | solution.py:40
  575.6 7.3 fusion.14
  583.5 37.0 %all_to_all.213 = f32[16,256,128]{2,1,0:T(8,128)} all-to-all(f32[16,256,128]{2,1,0:T(8,128)S(1)} %broadcast_in_dim.212), channel_id=1, replica_groups=mesh['row_0'=2,'row_1'=4,'row_2'=2,'col_0'=4,'col_1'=2] {'row_0','row_1'..., dimensions={0} | all-to-all | bytes 4194304 | tf_op jit(solution)/shard_map/all_to_all | solution.py:23
  625.1 7.9 all_to_all.214
  664.2 11.9 %fusion.12 = f32[96,1,128]{2,1,0:T(1,128)S(1)} fusion(f32[96,128,1]{1,2,0:T(1,128)} %bitcast.336, f32[96,1,128,128]{3,2,1,0:T(8,128)} %param.22), kind=kOutput, calls=%fused_computation.46 | convolution fusion | flops 18874368 | bytes 6389760 | tf_op jit(solution)/shard_map/kij,kj->ki/dot_general | solution.py:40
  678.7 5.6 all-to-all-start.26
  699.9 7.3 fusion.10
  707.8 36.6 %all_to_all.215 = f32[16,256,128]{2,1,0:T(8,128)} all-to-all(f32[16,256,128]{2,1,0:T(8,128)S(1)} %broadcast_in_dim.217), channel_id=1, replica_groups=mesh['row_0'=2,'row_1'=4,'row_2'=2,'col_0'=4,'col_1'=2] {'row_0','row_1'..., dimensions={0} | all-to-all | bytes 4194304 | tf_op jit(solution)/shard_map/all_to_all | solution.py:23
  749.1 7.8 all_to_all.216
  788.3 11.9 %fusion.8 = f32[96,1,128]{2,1,0:T(1,128)S(1)} fusion(f32[96,128,1]{1,2,0:T(1,128)} %bitcast.337, f32[96,1,128,128]{3,2,1,0:T(8,128)} %param.22), kind=kOutput, calls=%fused_computation.42 | convolution fusion | flops 18874368 | bytes 6389760 | tf_op jit(solution)/shard_map/kij,kj->ki/dot_general | solution.py:40
  823.7 7.3 fusion.6
  831.6 36.8 %all_to_all.217 = f32[16,256,128]{2,1,0:T(8,128)} all-to-all(f32[16,256,128]{2,1,0:T(8,128)S(1)} %broadcast_in_dim.222), channel_id=1, replica_groups=mesh['row_0'=2,'row_1'=4,'row_2'=2,'col_0'=4,'col_1'=2] {'row_0','row_1'..., dimensions={0} | all-to-all | bytes 4194304 | tf_op jit(solution)/shard_map/all_to_all | solution.py:23
  873.1 7.8 all_to_all.218
  911.5 11.8 %fusion.4 = f32[96,1,128]{2,1,0:T(1,128)S(1)} fusion(f32[96,128,1]{1,2,0:T(1,128)S(1)} %bitcast.348, f32[96,1,128,128]{3,2,1,0:T(8,128)} %param.22), kind=kOutput, calls=%fused_computation.38 | convolution fusion | flops 18874368 | bytes 6389760 | tf_op jit(solution)/shard_map/kij,kj->ki/dot_general | solution.py:40
  929.9 11.8 %fusion.2 = f32[96,1,128]{2,1,0:T(1,128)S(1)} fusion(f32[96,128,1]{1,2,0:T(1,128)S(1)} %bitcast.347, f32[96,1,128,128]{3,2,1,0:T(8,128)} %param.22), kind=kOutput, calls=%fused_computation.36 | convolution fusion | flops 18874368 | bytes 6389760 | tf_op jit(solution)/shard_map/kij,kj->ki/dot_general | solution.py:40
  961.8 7.3 fusion
  969.8 36.9 %all_to_all.219 = f32[16,256,128]{2,1,0:T(8,128)S(1)} all-to-all(f32[16,256,128]{2,1,0:T(8,128)S(1)} %broadcast_in_dim.227), channel_id=1, replica_groups=mesh['row_0'=2,'row_1'=4,'row_2'=2,'col_0'=4,'col_1'=2] {'row_0','row_1'..., dimensions={0} | all-to-all | bytes 4194304 | tf_op jit(solution)/shard_map/all_to_all | solution.py:23
  1007.5 5.9 all-reduce.4
  1013.4 8.4 all-reduce.1
  1021.7 6.0 all-reduce.3
  1027.8 7.2 all-reduce
  (382 shorter events, 386.2 us)
Async XLA Ops:
  0.6 18.1 %copy-start.5 = (f32[256,128]{1,0:T(8,128)S(1)}, f32[256,128]{1,0:T(8,128)}, u32[]{:S(2)}) copy-start(f32[256,128]{1,0:T(8,128)} %param.32) | copy-start | bytes 393220
  0.7 17.5 %copy-start.24 = (s32[96,1]{0,1:T(1,128)S(1)}, s32[96,1]{0,1:T(1,128)}, u32[]{:S(2)}) copy-start(s32[96,1]{0,1:T(1,128)} %param.24) | copy-start | bytes 1156
  1.4 18.1 %copy-start.38 = (pred[48]{0:T(512)(128)(4,1)}, pred[48]{0:T(512)(128)(4,1)S(1)}, u32[]{:S(2)}) copy-start(pred[48]{0:T(512)(128)(4,1)S(1)} %compare_and_fusion.1) | copy-start | bytes 148
  11.3 25.2 %all-to-all-start.2 = ((f32[8,64,128]{2,1,0:T(8,128)}), f32[8,64,128]{2,1,0:T(8,128)S(1)}, u32[]{:S(2)}, u32[]{:S(2)}) async-start(f32[8,64,128]{2,1,0:T(8,128)} %broadcast_in_dim.191), calls=%async_computation.2 | async-start | bytes 524288 | tf_op jit(solution)/shard_map/all_to_all | solution.py:23
  36.5 21.0 %copy-start.10 = (f32[8,64,128]{2,1,0:T(8,128)}, f32[8,64,128]{2,1,0:T(8,128)S(1)}, u32[]{:S(2)}) copy-start(f32[8,64,128]{2,1,0:T(8,128)S(1)} %all-to-all-done.2) | copy-start | bytes 786436
  38.4 16.7 %all-to-all-start.1 = ((f32[8,192,128]{2,1,0:T(8,128)}), f32[8,192,128]{2,1,0:T(8,128)}, u32[]{:S(2)}, u32[]{:S(2)}) async-start(f32[8,192,128]{2,1,0:T(8,128)} %broadcast_in_dim.190), calls=%async_computation.1 | async-start | bytes 1572864 | tf_op jit(solution)/shard_map/all_to_all | solution.py:23
  57.5 37.6 %all-to-all-start.4 = ((f32[16,256,128]{2,1,0:T(8,128)}), f32[16,256,128]{2,1,0:T(8,128)}, u32[]{:S(2)}, u32[]{:S(2)}) async-start(f32[16,256,128]{2,1,0:T(8,128)} %broadcast_in_dim.193), calls=%async_computation.4 | async-start | bytes 4194304 | tf_op jit(solution)/shard_map/all_to_all | solution.py:23
  96.7 35.4 %all-to-all-start = ((f32[16,256,128]{2,1,0:T(8,128)}), f32[16,256,128]{2,1,0:T(8,128)}, u32[]{:S(2)}, u32[]{:S(2)}) async-start(f32[16,256,128]{2,1,0:T(8,128)} %broadcast_in_dim.189), calls=%async_computation | async-start | bytes 4194304 | tf_op jit(solution)/shard_map/all_to_all | solution.py:23
  133.7 35.6 %all-to-all-start.3 = ((f32[16,256,128]{2,1,0:T(8,128)}), f32[16,256,128]{2,1,0:T(8,128)}, u32[]{:S(2)}, u32[]{:S(2)}) async-start(f32[16,256,128]{2,1,0:T(8,128)} %broadcast_in_dim.192), calls=%async_computation.3 | async-start | bytes 4194304 | tf_op jit(solution)/shard_map/all_to_all | solution.py:23
  141.0 30.6 %copy-start.2 = (f32[256,128]{1,0:T(8,128)S(1)}, f32[256,128]{1,0:T(8,128)}, u32[]{:S(2)}) copy-start(f32[256,128]{1,0:T(8,128)} %param.28) | copy-start | bytes 393220
  143.4 31.5 %copy-start.39 = (pred[48]{0:T(512)(128)(4,1)S(1)}, pred[48]{0:T(512)(128)(4,1)}, u32[]{:S(2)}) copy-start(pred[48]{0:T(512)(128)(4,1)} %copy-done.38) | copy-start | bytes 148
  145.7 34.4 %copy-start.43 = (pred[96]{0:T(512)(128)(4,1)S(1)}, pred[96]{0:T(512)(128)(4,1)}, u32[]{:S(2)}) copy-start(pred[96]{0:T(512)(128)(4,1)} %copy-done.42) | copy-start | bytes 292
  173.4 93.5 %copy-start.4 = (f32[256,128]{1,0:T(8,128)}, f32[256,128]{1,0:T(8,128)S(1)}, u32[]{:S(2)}) copy-start(f32[256,128]{1,0:T(8,128)S(1)} %get-tuple-element.47) | copy-start | bytes 393220
  180.9 16.1 %all-to-all-start.7 = ((f32[8,64,128]{2,1,0:T(8,128)}), f32[8,64,128]{2,1,0:T(8,128)}, u32[]{:S(2)}, u32[]{:S(2)}) async-start(f32[8,64,128]{2,1,0:T(8,128)} %broadcast_in_dim.196), calls=%async_computation.7 | async-start | bytes 524288 | tf_op jit(solution)/shard_map/all_to_all | solution.py:23
  185.0 20.2 %copy-start.47 = (pred[48]{0:T(512)(128)(4,1)S(1)}, pred[48]{0:T(512)(128)(4,1)}, u32[]{:S(2)}) copy-start(pred[48]{0:T(512)(128)(4,1)} %copy-done.46) | copy-start | bytes 148
  198.0 17.0 %all-to-all-start.6 = ((f32[8,192,128]{2,1,0:T(8,128)}), f32[8,192,128]{2,1,0:T(8,128)}, u32[]{:S(2)}, u32[]{:S(2)}) async-start(f32[8,192,128]{2,1,0:T(8,128)} %broadcast_in_dim.195), calls=%async_computation.6 | async-start | bytes 1572864 | tf_op jit(solution)/shard_map/all_to_all | solution.py:23
  227.2 61.4 %copy-start.7 = (f32[256,128]{1,0:T(8,128)S(1)}, f32[256,128]{1,0:T(8,128)}, u32[]{:S(2)}) copy-start(f32[256,128]{1,0:T(8,128)} %get-tuple-element.48) | copy-start | bytes 393220
  264.5 27.2 %copy-start.40 = (pred[48]{0:T(512)(128)(4,1)S(1)}, pred[48]{0:T(512)(128)(4,1)}, u32[]{:S(2)}) copy-start(pred[48]{0:T(512)(128)(4,1)} %copy-done.38) | copy-start | bytes 148
  266.9 29.9 %copy-start.34 = (s32[48,1]{0,1:T(1,128)S(1)}, s32[48,1]{0,1:T(1,128)}, u32[]{:S(2)}) copy-start(s32[48,1]{0,1:T(1,128)} %param.26) | copy-start | bytes 580
  266.9 30.0 %copy-start.44 = (pred[96]{0:T(512)(128)(4,1)S(1)}, pred[96]{0:T(512)(128)(4,1)}, u32[]{:S(2)}) copy-start(pred[96]{0:T(512)(128)(4,1)} %copy-done.42) | copy-start | bytes 292
  278.4 8.2 all-to-all-start.9
  297.7 16.3 %all-to-all-start.12 = ((f32[8,64,128]{2,1,0:T(8,128)}), f32[8,64,128]{2,1,0:T(8,128)}, u32[]{:S(2)}, u32[]{:S(2)}) async-start(f32[8,64,128]{2,1,0:T(8,128)} %broadcast_in_dim.201), calls=%async_computation.12 | async-start | bytes 524288 | tf_op jit(solution)/shard_map/all_to_all | solution.py:23
  301.9 19.8 %copy-start.48 = (pred[48]{0:T(512)(128)(4,1)S(1)}, pred[48]{0:T(512)(128)(4,1)}, u32[]{:S(2)}) copy-start(pred[48]{0:T(512)(128)(4,1)} %copy-done.46) | copy-start | bytes 148
  315.0 14.3 %all-to-all-start.11 = ((f32[8,192,128]{2,1,0:T(8,128)}), f32[8,192,128]{2,1,0:T(8,128)}, u32[]{:S(2)}, u32[]{:S(2)}) async-start(f32[8,192,128]{2,1,0:T(8,128)} %broadcast_in_dim.200), calls=%async_computation.11 | async-start | bytes 1572864 | tf_op jit(solution)/shard_map/all_to_all | solution.py:23
  377.9 29.2 %copy-start.41 = (pred[48]{0:T(512)(128)(4,1)S(1)}, pred[48]{0:T(512)(128)(4,1)}, u32[]{:S(2)}) copy-start(pred[48]{0:T(512)(128)(4,1)} %copy-done.38) | copy-start | bytes 148
  379.6 22.5 %copy-start.9 = (f32[256,128]{1,0:T(8,128)}, f32[256,128]{1,0:T(8,128)S(1)}, u32[]{:S(2)}) copy-start(f32[256,128]{1,0:T(8,128)S(1)} %reduce_sum.495) | copy-start | bytes 393220
  379.6 33.3 %copy-start.35 = (s32[48,1]{0,1:T(1,128)S(1)}, s32[48,1]{0,1:T(1,128)}, u32[]{:S(2)}) copy-start(s32[48,1]{0,1:T(1,128)} %param.26) | copy-start | bytes 580
  391.2 8.9 all-to-all-start.14
  404.5 97.9 %copy-start.3 = (f32[256,128]{1,0:T(8,128)}, f32[256,128]{1,0:T(8,128)S(1)}, u32[]{:S(2)}) copy-start(f32[256,128]{1,0:T(8,128)S(1)} %get-tuple-element.42) | copy-start | bytes 393220
  415.2 17.6 %all-to-all-start.17 = ((f32[8,64,128]{2,1,0:T(8,128)}), f32[8,64,128]{2,1,0:T(8,128)}, u32[]{:S(2)}, u32[]{:S(2)}) async-start(f32[8,64,128]{2,1,0:T(8,128)} %broadcast_in_dim.206), calls=%async_computation.17 | async-start | bytes 524288 | tf_op jit(solution)/shard_map/all_to_all | solution.py:23
  434.6 15.1 %all-to-all-start.16 = ((f32[8,192,128]{2,1,0:T(8,128)}), f32[8,192,128]{2,1,0:T(8,128)}, u32[]{:S(2)}, u32[]{:S(2)}) async-start(f32[8,192,128]{2,1,0:T(8,128)} %broadcast_in_dim.205), calls=%async_computation.16 | async-start | bytes 1572864 | tf_op jit(solution)/shard_map/all_to_all | solution.py:23
  513.3 8.2 all-to-all-start.19
  536.1 16.9 %all-to-all-start.22 = ((f32[8,64,128]{2,1,0:T(8,128)}), f32[8,64,128]{2,1,0:T(8,128)}, u32[]{:S(2)}, u32[]{:S(2)}) async-start(f32[8,64,128]{2,1,0:T(8,128)} %broadcast_in_dim.211), calls=%async_computation.22 | async-start | bytes 524288 | tf_op jit(solution)/shard_map/all_to_all | solution.py:23
  554.8 14.2 %all-to-all-start.21 = ((f32[8,192,128]{2,1,0:T(8,128)}), f32[8,192,128]{2,1,0:T(8,128)}, u32[]{:S(2)}, u32[]{:S(2)}) async-start(f32[8,192,128]{2,1,0:T(8,128)} %broadcast_in_dim.210), calls=%async_computation.21 | async-start | bytes 1572864 | tf_op jit(solution)/shard_map/all_to_all | solution.py:23
  634.2 9.0 all-to-all-start.24
  660.1 16.8 %all-to-all-start.27 = ((f32[8,64,128]{2,1,0:T(8,128)}), f32[8,64,128]{2,1,0:T(8,128)}, u32[]{:S(2)}, u32[]{:S(2)}) async-start(f32[8,64,128]{2,1,0:T(8,128)} %broadcast_in_dim.216), calls=%async_computation.27 | async-start | bytes 524288 | tf_op jit(solution)/shard_map/all_to_all | solution.py:23
  678.7 14.7 %all-to-all-start.26 = ((f32[8,192,128]{2,1,0:T(8,128)}), f32[8,192,128]{2,1,0:T(8,128)}, u32[]{:S(2)}, u32[]{:S(2)}) async-start(f32[8,192,128]{2,1,0:T(8,128)} %broadcast_in_dim.215), calls=%async_computation.26 | async-start | bytes 1572864 | tf_op jit(solution)/shard_map/all_to_all | solution.py:23
  758.2 8.9 all-to-all-start.29
  784.1 17.0 %all-to-all-start.32 = ((f32[8,64,128]{2,1,0:T(8,128)}), f32[8,64,128]{2,1,0:T(8,128)}, u32[]{:S(2)}, u32[]{:S(2)}) async-start(f32[8,64,128]{2,1,0:T(8,128)} %broadcast_in_dim.221), calls=%async_computation.32 | async-start | bytes 524288 | tf_op jit(solution)/shard_map/all_to_all | solution.py:23
  802.9 14.3 %all-to-all-start.31 = ((f32[8,192,128]{2,1,0:T(8,128)}), f32[8,192,128]{2,1,0:T(8,128)}, u32[]{:S(2)}, u32[]{:S(2)}) async-start(f32[8,192,128]{2,1,0:T(8,128)} %broadcast_in_dim.220), calls=%async_computation.31 | async-start | bytes 1572864 | tf_op jit(solution)/shard_map/all_to_all | solution.py:23
  882.2 9.1 all-to-all-start.34
  895.9 15.5 %copy-start.45 = (pred[96]{0:T(512)(128)(4,1)S(1)}, pred[96]{0:T(512)(128)(4,1)}, u32[]{:S(2)}) copy-start(pred[96]{0:T(512)(128)(4,1)} %copy-done.42) | copy-start | bytes 292
  907.3 16.2 %all-to-all-start.37 = ((f32[8,64,128]{2,1,0:T(8,128)}), f32[8,64,128]{2,1,0:T(8,128)}, u32[]{:S(2)}, u32[]{:S(2)}) async-start(f32[8,64,128]{2,1,0:T(8,128)} %broadcast_in_dim.226), calls=%async_computation.37 | async-start | bytes 524288 | tf_op jit(solution)/shard_map/all_to_all | solution.py:23
  924.5 17.5 %all-to-all-start.35 = ((f32[8,192,128]{2,1,0:T(8,128)}), f32[8,192,128]{2,1,0:T(8,128)}, u32[]{:S(2)}, u32[]{:S(2)}) async-start(f32[8,192,128]{2,1,0:T(8,128)} %broadcast_in_dim.224), calls=%async_computation.35 | async-start | bytes 1572864 | tf_op jit(solution)/shard_map/all_to_all | solution.py:23
  929.9 19.9 %copy-start.49 = (pred[48]{0:T(512)(128)(4,1)S(1)}, pred[48]{0:T(512)(128)(4,1)}, u32[]{:S(2)}) copy-start(pred[48]{0:T(512)(128)(4,1)} %copy-done.46) | copy-start | bytes 148
  942.9 14.2 %all-to-all-start.36 = ((f32[8,192,128]{2,1,0:T(8,128)}), f32[8,192,128]{2,1,0:T(8,128)}, u32[]{:S(2)}, u32[]{:S(2)}) async-start(f32[8,192,128]{2,1,0:T(8,128)} %broadcast_in_dim.225), calls=%async_computation.36 | async-start | bytes 1572864 | tf_op jit(solution)/shard_map/all_to_all | solution.py:23
  969.8 37.1 %copy-start.6 = (f32[256,128]{1,0:T(8,128)S(1)}, f32[256,128]{1,0:T(8,128)}, u32[]{:S(2)}) copy-start(f32[256,128]{1,0:T(8,128)} %get-tuple-element.33) | copy-start | bytes 393220
  969.8 37.1 %copy-start.12 = (f32[256,128]{1,0:T(8,128)S(1)}, f32[256,128]{1,0:T(8,128)}, u32[]{:S(2)}) copy-start(f32[256,128]{1,0:T(8,128)} %param.29) | copy-start | bytes 393220
  (32 other events, 270.8 us)
where the time goes:
time: 1060 us; the launch traced here: 1040 us
  blocking collectives  335 us (32%)
  matrix products  253 us (24%)
  starting transfers between devices  131 us (12%)
  other arithmetic  117 us (11%)
  waiting for transfers between devices  92.9 us (9%)
  local copies, waits for them, and re-layouts  86.3 us (8%)
  between operations  24.4 us (2%)
    all_to_all x13, blocking collectives, sent_to_all(): return lax.all_to_all(copies, axis, split_axis=0, concat_axis=0, tiled=True)  303 us
    dot_general x17, matrix products, forward_tiles(): jnp.einsum('kij,kj->ki', tiles, jnp.take(vec, cols, axis=0), precision=HIGH)  150 us
    all_to_all x26, starting transfers between devices, sent_to_all(): return lax.all_to_all(copies, axis, split_axis=0, concat_axis=0, tiled=True)  131 us
    all_to_all x26, waiting for transfers between devices, sent_to_all(): return lax.all_to_all(copies, axis, split_axis=0, concat_axis=0, tiled=True)  92.9 us
    dot_general x17, matrix products, backward_tiles(): jnp.einsum('kij,ki->kj', tiles, jnp.take(vec, rows, axis=0), precision=HIGH)  91.5 us
    reduce_sum x39, other arithmetic, over_copies(): return sent_to_all(shard, axis).sum(axis=0)  58.3 us
    broadcast_in_dim x39, local copies, waits for them, and re-layouts, sent_to_all(): copies = jnp.broadcast_to(shard, (lax.axis_size(axis), *shard.shape))  36.9 us
    pmax x5, blocking collectives, over_axes(): return functools.reduce(lax.pmax, axes, shard)  31.9 us
  transfers between devices with their start and end apart: 26, of which 17 were waited for; matrix products, arithmetic and copies ran while one was open for 19% of the time, Pallas kernels for 0%

commit v1 on v0

v1 whole, which is shorter than its diff:
```python
import functools

import jax
import jax.numpy as jnp
from jax import lax
from jax.experimental import pallas as pl
from jax.experimental.pallas import tpu as pltpu
from jax.sharding import PartitionSpec as P

MESH = pl.DeviceIdType.MESH
YG = 64
CG = 6
SIGMA = 1e-06
RELAX = 1.6
B = 128
TPG = 16
F32 = jnp.float32
BF16 = jnp.bfloat16


def ring_distance(step, size):
    return min(step, size - step)


def peer_offsets(dims, weights):
    offsets = [()]
    for size in dims:
        offsets = [o + (s,) for o in offsets for s in range(size)]
    cost = lambda o: sum(w * ring_distance(s, n) for s, n, w in zip(o, dims, weights))
    return sorted([o for o in offsets if any(o)], key=cost, reverse=True)


def shifted(index, offset, dims, sign):
    out, stride = 0, 1
    for size, step in reversed(list(zip(dims, offset))):
        coord = lax.rem(lax.div(index, jnp.int32(stride)), jnp.int32(size))
        move = step if sign > 0 else (size - step) % size
        coord = lax.rem(coord + jnp.int32(move), jnp.int32(size))
        out = out + coord * jnp.int32(stride)
        stride *= size
    return out


def halves(value):
    high = value.astype(BF16)
    return high, (value - high.astype(F32)).astype(BF16)


def dot(a, b):
    return lax.dot_general(a, b, (((1,), (0,)), ((), ())), preferred_element_type=F32)


class Exchange:
    def __init__(self, axis, index, dims, offsets, sems):
        self.axis, self.index, self.dims, self.offsets, self.sems = axis, index, dims, offsets, sems

    def copy(self, k, src, dst, peer):
        return pltpu.make_async_remote_copy(
            src_ref=src,
            dst_ref=dst,
            send_sem=self.sems.at[0, k],
            recv_sem=self.sems.at[1, k],
            device_id={self.axis: peer},
            device_id_type=MESH,
        )

    def start(self, src_of, dst_of):
        for k, off in enumerate(self.offsets):
            peer = shifted(self.index, off, self.dims, 1)
            self.copy(k, src_of(peer), dst_of(peer), peer).start()

    def wait(self, src_of, dst_from):
        for k, off in enumerate(self.offsets):
            sender = shifted(self.index, off, self.dims, -1)
            self.copy(k, dst_from(sender), dst_from(sender), sender).wait_recv()
        for k, off in enumerate(self.offsets):
            peer = shifted(self.index, off, self.dims, 1)
            self.copy(k, src_of(peer), src_of(peer), peer).wait_send()


def kernel(cfg, ct, ft, idx, diag_in, q_in, x0_in, lb, ub, z0, y0, rho_ref,
           pn_o, sl_o, du_o, res_o,
           raw, tiles, ohc, ohct, ohr, ohrt, lanes_a, lanes_b, part, sqpart,
           ufull, yfull, pfull, xfull, yp, yx, ystart, x0t, prec, dfull, qt, rsh, ssh,
           rcv_c, rcv_r, rcv_q, scal_c, scal_r, scal_m, scal_n,
           load_sems, sem_rc, sem_ac, sem_sc, sem_rr, sem_ar, sem_sr, sem_q, sem_aq, sem_m, sem_n):
    nr, nc, ga, gg, rdims, cdims, roffs, coffs, yb = cfg
    ng = ga + gg
    row = lax.axis_index("row")
    col = lax.axis_index("col")
    jr, ic = B // nr, B // nc
    xw = ufull.shape[1]
    rho = rho_ref[0, 0]

    barrier = pltpu.get_barrier_semaphore()
    for off in roffs:
        pl.semaphore_signal(barrier, inc=1, device_id={"row": shifted(row, off, rdims, 1)}, device_id_type=MESH)
    for off in coffs:
        pl.semaphore_signal(barrier, inc=1, device_id={"col": shifted(col, off, cdims, 1)}, device_id_type=MESH)

    def load(g):
        src = ct.at[pl.ds(g * TPG, TPG)] if g < ga else ft.at[pl.ds((g - ga) * TPG, TPG)]
        return pltpu.make_async_copy(src, raw.at[g], load_sems.at[g])

    for g in range(ng):
        load(g).start()

    def ex(axis, sems):
        if axis == "row":
            return Exchange("row", row, rdims, roffs, sems)
        return Exchange("col", col, cdims, coffs, sems)

    x_rc, x_ac, x_sc = ex("col", sem_rc), ex("col", sem_ac), ex("col", sem_sc)
    x_rr, x_ar, x_sr = ex("row", sem_rr), ex("row", sem_ar), ex("row", sem_sr)
    x_q, x_aq, x_m, x_n = ex("row", sem_q), ex("row", sem_aq), ex("row", sem_m), ex("col", sem_n)

    jrows = lambda i: pl.ds(pl.multiple_of(i * jr, jr), jr)
    irows = lambda i: pl.ds(pl.multiple_of(i * ic, ic), ic)
    mine_j, mine_i = jrows(row), irows(col)

    def transposed(ref, dst):
        for b in range(xw // B):
            dst[:, b * B:(b + 1) * B] = ref[b * B:(b + 1) * B, :].T

    transposed(x0_in, x0t)
    transposed(diag_in, dfull)
    transposed(q_in, qt)

    def onehots(g, _):
        at = pl.ds(pl.multiple_of(g * B, B), B)
        for which, (oh, oht) in enumerate(((ohc, ohct), (ohr, ohrt))):
            ids = jnp.broadcast_to(idx[which, pl.ds(g, 1), :], (B, B))
            wide = jnp.concatenate([ids] * (xw // B), axis=0)
            blocks = lax.broadcasted_iota(jnp.int32, (xw, B), 0).astype(F32)
            oh[:, at] = jnp.where(wide == blocks, 1.0, 0.0).astype(BF16)
            tall = jnp.concatenate([ids.T] * (xw // B), axis=1)
            blocks = lax.broadcasted_iota(jnp.int32, (B, xw), 1).astype(F32)
            oht[at, :] = jnp.where(tall == blocks, 1.0, 0.0).astype(BF16)
        return 0

    lax.fori_loop(0, ng, onehots, 0)

    mask = jnp.where(
        lax.rem(lax.broadcasted_iota(jnp.int32, (8, B), 1), jnp.int32(8)) == lax.broadcasted_iota(jnp.int32, (8, B), 0),
        1.0, 0.0).astype(F32)

    def relayout(g, _):
        pltpu.make_async_copy(ct.at[pl.ds(0, TPG)], raw.at[g], load_sems.at[g]).wait()
        total = jnp.zeros((B, B), F32)
        for i in range(B // 8):
            block = raw[g, :, 8 * i:8 * i + 8, :].reshape(B, B).T
            tiles[g, i] = block
            total = total + block * block
        at = pl.ds(pl.multiple_of(g * B, B), B)
        lanes_b[:, at] = total * jnp.where(g < ga, rho, 1.0)
        return 0

    lax.fori_loop(0, ng, relayout, 0)

    def scatter(lanes, onehot_t, dst):
        high, low = halves(lanes[...])
        dst[...] = dot(high, onehot_t[...]) + dot(low, onehot_t[...])

    def gather(value, onehot, lanes):
        high, low = halves(value)
        lanes[...] = dot(high, onehot[...]) + dot(low, onehot[...])

    def forward(value):
        gather(value, ohc, lanes_a)

        def body(g, _):
            at = pl.ds(pl.multiple_of(g * B, B), B)
            v = lanes_a[:, at]
            for i in range(B // 8):
                prod = (tiles[g, i] * v).reshape(B // 8, 8, B).sum(axis=0)
                lanes_b[8 * i:8 * i + 8, at] = prod.sum(axis=0, keepdims=True) * mask
            return 0

        lax.fori_loop(0, ng, body, 0)
        scatter(lanes_b, ohrt, part)

    def backward(value):
        gather(value, ohr, lanes_a)

        def body(g, _):
            at = pl.ds(pl.multiple_of(g * B, B), B)
            us = [(lanes_a[8 * i:8 * i + 8, at] * mask).sum(axis=0, keepdims=True) for i in range(B // 8)]
            us = [jnp.broadcast_to(u, (8, B)) for u in us]
            for j in range(B // 8):
                acc = tiles[g, 0, 8 * j:8 * j + 8, :] * us[0]
                for i in range(1, B // 8):
                    acc = acc + tiles[g, i, 8 * j:8 * j + 8, :] * us[i]
                lanes_b[8 * j:8 * j + 8, at] = acc
            return 0

        lax.fori_loop(0, ng, body, 0)
        scatter(lanes_b, ohct, part)

    lane_x = lax.broadcasted_iota(jnp.int32, (1, xw), 1)
    weight = jnp.where(lane_x < yb, rho, 1.0)

    def fold(value):
        s = value.sum(axis=0, keepdims=True)
        out = s[:, :B]
        for b in range(1, xw // B):
            out = out + s[:, b * B:(b + 1) * B]
        return out

    def fold_max(value):
        s = value.max(axis=0, keepdims=True)
        out = s[:, :B]
        for b in range(1, xw // B):
            out = jnp.maximum(out, s[:, b * B:(b + 1) * B])
        return out

    def start_rc():
        x_rc.start(lambda p: part.at[irows(p)], lambda p: rcv_c.at[col])

    def finish_rc():
        x_rc.wait(lambda p: part.at[irows(p)], lambda s: rcv_c.at[s])
        total = part[mine_i, :]
        for off in coffs:
            total = total + rcv_c[shifted(col, off, cdims, -1)]
        yfull[mine_i, :] = total
        x_ac.start(lambda p: yfull.at[mine_i], lambda p: yfull.at[mine_i])

    def finish_ac():
        x_ac.wait(lambda p: yfull.at[mine_i], lambda s: yfull.at[irows(s)])

    def start_rr():
        x_rr.start(lambda p: part.at[jrows(p)], lambda p: rcv_r.at[row])

    def finish_rr():
        x_rr.wait(lambda p: part.at[jrows(p)], lambda s: rcv_r.at[s])
        total = part[mine_j, :]
        for off in roffs:
            total = total + rcv_r[shifted(row, off, rdims, -1)]
        return total

    def start_ar(u):
        ufull[mine_j, :] = u
        x_ar.start(lambda p: ufull.at[mine_j], lambda p: ufull.at[mine_j])

    def finish_ar():
        x_ar.wait(lambda p: ufull.at[mine_j], lambda s: ufull.at[jrows(s)])

    scatter(lanes_b, ohct, sqpart)
    pl.semaphore_wait(barrier, len(roffs) + len(coffs))
    x_q.start(lambda p: sqpart.at[jrows(p)], lambda p: rcv_q.at[row])

    forward(x0t[...])
    start_rc()
    x_q.wait(lambda p: sqpart.at[jrows(p)], lambda s: rcv_q.at[s])
    total = sqpart[mine_j, :] + dfull[mine_j, :] + SIGMA
    for off in roffs:
        total = total + rcv_q[shifted(row, off, rdims, -1)]
    prec[mine_j, :] = total
    x_aq.start(lambda p: prec.at[mine_j], lambda p: prec.at[mine_j])

    first = rho * z0[...] - y0[...]
    first = jnp.concatenate([first, jnp.zeros((xw - yb, B), F32)], axis=0)
    for b in range(xw // B):
        yx[:, b * B:(b + 1) * B] = first[b * B:(b + 1) * B, :].T
    finish_rc()
    finish_ac()
    ystart[...] = yfull[...]
    backward(yx[...] - weight * yfull[...])
    start_rr()
    x_aq.wait(lambda p: prec.at[mine_j], lambda s: prec.at[jrows(s)])
    xfull[...] = x0t[...]
    pfull[...] = jnp.zeros_like(pfull)
    yp[...] = jnp.zeros_like(yp)
    yx[...] = ystart[...]
    ssh[...] = jnp.zeros_like(ssh)
    resid = finish_rr() - qt[mine_j, :] - dfull[mine_j, :] * x0t[mine_j, :]
    rsh[...] = resid
    start_ar(resid / prec[mine_j, :])
    finish_ar()

    def first_half(gamma, has_old):
        u = ufull[...]
        square = u * u
        scal_c[col, 0:1, :] = fold(prec[...] * square)
        scal_c[col, 1:2, :] = fold((dfull[...] + SIGMA) * square)
        x_sc.start(lambda p: scal_c.at[col], lambda p: scal_c.at[col])
        forward(u)
        start_rc()
        x_sc.wait(lambda p: scal_c.at[col], lambda s: scal_c.at[s])
        sums = scal_c[...].sum(axis=0)
        sums = sums.sum(axis=1, keepdims=True)
        gamma_new, dx = sums[0:1, :], sums[1:2, :]
        beta = jnp.where(has_old, gamma_new / gamma, 0.0)
        finish_rc()
        pfull[...] = u + beta * pfull[...]
        finish_ac()
        y = yfull[...]
        scal_r[row] = fold(weight * (y * y))
        x_sr.start(lambda p: scal_r.at[row], lambda p: scal_r.at[row])
        return gamma_new, dx, beta

    def step_length(gamma_new, dx, beta, alpha):
        x_sr.wait(lambda p: scal_r.at[row], lambda s: scal_r.at[s])
        delta = dx + scal_r[...].sum(axis=0).sum(axis=1, keepdims=True)
        return gamma_new / (delta - beta * gamma_new / alpha)

    def follow(alpha, beta):
        xfull[...] = xfull[...] + alpha * pfull[...]
        y = yfull[...] + beta * yp[...]
        yp[...] = y
        yx[...] = yx[...] + alpha * y

    def step(t, carry):
        gamma, alpha = carry
        gamma_new, dx, beta = first_half(gamma, t > 0)
        backward(weight * yfull[...])
        start_rr()
        alpha = step_length(gamma_new, dx, beta, alpha)
        u = ufull[mine_j, :]
        image = finish_rr() + (dfull[mine_j, :] + SIGMA) * u
        along = image + beta * ssh[...]
        ssh[...] = along
        resid = rsh[...] - alpha * along
        rsh[...] = resid
        start_ar(resid / prec[mine_j, :])
        follow(alpha, beta)
        finish_ar()
        return gamma_new, alpha

    one = jnp.ones((1, 1), F32)
    gamma, alpha = lax.fori_loop(0, CG - 1, step, (one, one))
    gamma, dx, beta = first_half(gamma, True)
    alpha = step_length(gamma, dx, beta, alpha)
    follow(alpha, beta)

    for b in range(xw // B):
        at = slice(b * B, (b + 1) * B)
        ystart_t = ystart[:, at].T
        yx_t = yx[:, at].T
        rows = min(yb - b * B, B)
        zt = yx_t[:rows]
        rs = slice(b * B, b * B + rows)
        relaxed = RELAX * zt + (1.0 - RELAX) * z0[rs, :]
        dual = y0[rs, :]
        slack = jnp.minimum(jnp.maximum(relaxed + dual / rho, lb[rs, :]), ub[rs, :])
        dual = dual + rho * (relaxed - slack)
        sl_o[rs, :] = slack
        du_o[rs, :] = dual
        image = RELAX * yx_t + (1.0 - RELAX) * ystart_t
        gap = jnp.abs(image[:rows] - slack).max(axis=0, keepdims=True)
        primal = gap if b == 0 else jnp.maximum(primal, gap)
        if rows < B:
            dual = jnp.concatenate([dual, image[rows:]], axis=0)
        yp[:, at] = dual.T
    backward(yp[...])
    start_rr()
    pfull[...] = RELAX * xfull[...] + (1.0 - RELAX) * x0t[...]
    for b in range(xw // B):
        pn_o[b * B:(b + 1) * B, :] = pfull[:, b * B:(b + 1) * B].T
    dvec = finish_rr() + dfull[mine_j, :] * pfull[mine_j, :] + qt[mine_j, :]
    scal_m[row, 0:1, :] = primal
    scal_m[row, 1:2, :] = fold_max(jnp.abs(dvec))
    x_m.start(lambda p: scal_m.at[row], lambda p: scal_m.at[row])
    x_m.wait(lambda p: scal_m.at[row], lambda s: scal_m.at[s])
    scal_n[col] = scal_m[...].max(axis=0)
    x_n.start(lambda p: scal_n.at[col], lambda p: scal_n.at[col])
    x_n.wait(lambda p: scal_n.at[col], lambda s: scal_n.at[s])
    worst = scal_n[...].max(axis=0).max(axis=1, keepdims=True)
    res_o[...] = jnp.broadcast_to(worst, res_o.shape)


def local(dims, ct, crow, ccol, ft, frow, fcol, diag, q, lb, ub, x0, z0, y0, penalty):
    nr, nc, rdims, cdims, rweights, cweights = dims
    ka, kg = ct.shape[0], ft.shape[0]
    ct, ft = ct.reshape(ka, B, B), ft.reshape(kg, B, B)
    ga, gg = ka // TPG, kg // TPG
    ng = ga + gg
    yb = z0.shape[0]
    xw = x0.shape[0]
    cols = jnp.concatenate([ccol.reshape(-1), fcol.reshape(-1)])
    rows = jnp.concatenate([crow.reshape(-1), frow.reshape(-1) + yb])
    idx = jnp.repeat(jnp.stack([cols, rows]).astype(F32), 8, axis=1).reshape(2, ng, B)
    roffs = peer_offsets(rdims, rweights)
    coffs = peer_offsets(cdims, cweights)
    cfg = (nr, nc, ga, gg, rdims, cdims, roffs, coffs, yb)
    lanes = ng * B
    jr, ic = B // nr, B // nc
    vmem = pl.BlockSpec(memory_space=pltpu.VMEM)
    hbm = pl.BlockSpec(memory_space=pl.ANY)
    full = pltpu.VMEM((B, xw), F32)
    dma = pltpu.SemaphoreType.DMA
    csem, rsem = dma((2, len(coffs))), dma((2, len(roffs)))
    outs = pl.pallas_call(
        functools.partial(kernel, cfg),
        out_shape=(
            jax.ShapeDtypeStruct((xw, B), F32),
            jax.ShapeDtypeStruct((yb, B), F32),
            jax.ShapeDtypeStruct((yb, B), F32),
            jax.ShapeDtypeStruct((2, B), F32),
        ),
        in_specs=[hbm, hbm] + [vmem] * 8 + [pl.BlockSpec(memory_space=pltpu.SMEM)],
        out_specs=(vmem,) * 4,
        scratch_shapes=[
            pltpu.VMEM((ng, TPG, B, B), F32),
            pltpu.VMEM((ng, B // 8, B, B), F32),
            pltpu.VMEM((xw, lanes), BF16),
            pltpu.VMEM((lanes, xw), BF16),
            pltpu.VMEM((xw, lanes), BF16),
            pltpu.VMEM((lanes, xw), BF16),
            pltpu.VMEM((B, lanes), F32),
            pltpu.VMEM((B, lanes), F32),
            full, full,
            full, full, full, full, full, full, full, full, full, full, full,
            pltpu.VMEM((jr, xw), F32),
            pltpu.VMEM((jr, xw), F32),
            pltpu.VMEM((nc, ic, xw), F32),
            pltpu.VMEM((nr, jr, xw), F32),
            pltpu.VMEM((nr, jr, xw), F32),
            pltpu.VMEM((nc, 2, B), F32),
            pltpu.VMEM((nr, 1, B), F32),
            pltpu.VMEM((nr, 2, B), F32),
            pltpu.VMEM((nc, 2, B), F32),
            dma((ng,)),
            csem, csem, csem, rsem, rsem, rsem, rsem, rsem, rsem, csem,
        ],
        compiler_params=pltpu.CompilerParams(collective_id=0, has_side_effects=True),
    )(ct, ft, idx, diag, q, x0, lb, ub, z0, y0, penalty.reshape(1, 1))
    pn, sl, du, res = outs
    return pn, sl, du, res[0, 0], res[1, 0]


def solution(mesh):
    nr, nc = mesh.shape["row"], mesh.shape["col"]
    rdims, rweights = ((2, 4, 2), (2, 1, 0)) if nr == 16 else ((nr,), (1,))
    cdims, cweights = ((4, 2), (1, 1)) if nc == 8 else ((nc,), (1,))
    dims = (nr, nc, rdims, cdims, rweights, cweights)
    rc = P("row", "col")
    tiles = P("row", "col", None, None)
    xs, ys = P("col", None), P("row", None)
    return jax.shard_map(
        functools.partial(local, dims),
        mesh=mesh,
        in_specs=(tiles, rc, rc, tiles, rc, rc, xs, xs, ys, ys, xs, ys, ys, P()),
        out_specs=(xs, ys, ys, P(), P()),
        check_vma=False,
    )
```

time: 1060 us -> 184 us (0.17); the launches traced: 1040 us -> 184 us
  blocking collectives: 335 us -> 0 us
  matrix products: 253 us -> 0 us
  Pallas kernels: 0 us -> 174 us
  starting transfers between devices: 131 us -> 0 us
  other arithmetic: 117 us -> 2.14 us
  waiting for transfers between devices: 92.9 us -> 0 us
  local copies, waits for them, and re-layouts: 86.3 us -> 6.69 us
  between operations: 24.4 us -> 1.3 us
    all_to_all x13 -> x0, blocking collectives: 303 us -> none  [sent_to_all(): return lax.all_to_all(copies, axis, split_axis=0, concat_axis=0, tiled=True)]
    dot_general x70 -> x0, matrix products: 253 us -> none  [the longest x17 150 us: forward_tiles(): jnp.einsum('kij,kj->ki', tiles, jnp.take(vec, cols, axis=0), precision=HIGH)]
    pallas_call x0 -> x1, Pallas kernels: none -> 174 us  [local(): pl.pallas_call(functools.partial(kernel, cfg), out_shape=(jax.ShapeDtypeS...]
    all_to_all x26 -> x0, starting transfers between devices: 131 us -> none  [sent_to_all(): return lax.all_to_all(copies, axis, split_axis=0, concat_axis=0, tiled=True)]
    all_to_all x26 -> x0, waiting for transfers between devices: 92.9 us -> none  [sent_to_all(): return lax.all_to_all(copies, axis, split_axis=0, concat_axis=0, tiled=True)]
    reduce_sum x47 -> x0, other arithmetic: 70.8 us -> none  [the longest x39 58.3 us: over_copies(): return sent_to_all(shard, axis).sum(axis=0)]
    gather x34 -> x0, local copies, waits for them, and re-layouts: 48.6 us -> none  [the longest x17 24.5 us: backward_tiles(): jnp.take(vec, rows, axis=0)]
    broadcast_in_dim x39 -> x1, local copies, waits for them, and re-layouts: 36.9 us -> 0.09 us  [local(): jnp.repeat(jnp.stack([cols, rows]).astype(F32), 8, axis=1).reshape(2, ng, B)]
  transfers between devices with their start and end apart: 26 -> 0, of which waited for: 17 -> 0; matrix products, arithmetic and copies ran while one was open for 19% -> 0% of each run, Pallas kernels for 0% -> 0%
where the time goes in v1:
time: 184 us
  Pallas kernels  174 us (95%)
  local copies, waits for them, and re-layouts  6.69 us (4%)
  other arithmetic  2.14 us (1%)
    pallas_call x1, Pallas kernels, local(): pl.pallas_call(functools.partial(kernel, cfg), out_shape=(jax.ShapeDtypeS...  174 us
    unnamed x3, local copies, waits for them, and re-layouts  4.64 us

profile of v1, /device:TPU:1, one launch (start us, length us, event | category | flops | bytes accessed | tf_op | source)
XLA Modules:
  0.0 184.1 jit_solution(1897779355907596005)
XLA Ops:
  1.3 0.7 add_bitcast_fusion
  1.9 0.7 pad_add_fusion.1
  2.7 0.7 pad_add_fusion
  3.4 0.1 broadcast_in_dim.3
  3.5 0.7 reshape_reshape.3.idx
  4.3 174.0 %shard_map.173 = (f32[256,128]{1,0:T(8,128)}, f32[192,128]{1,0:T(8,128)}, f32[192,128]{1,0:T(8,128)}, f32[2,128]{1,0:T(2,128)}) custom-call(f32[96,128,128]{2,1,0:T(8,128)} %bitcast.13, f32[48,128,128]{2,1,0:T(8,128)} %bitcast.14, f32[2,9,128]{2,1,0:T(8,128)} %reshape_reshape.3.idx, f32[256,128]{1,0:T(8,128)} %diag_in.1, f32[256,128]{1,0:T(8,128)} %q_in.1, ...), custom_call_target="tpu_custom_call" | custom-call | tf_op jit(solution)/shard_map/pallas_call | solution.py:392
  178.2 1.2 fusion
  179.5 1.6 copy.23
  181.0 1.5 copy.24
  182.6 1.5 copy.25
  (1 shorter events, 0.0 us)

commit v2 on v1

v2 whole, which is shorter than its diff:
```python
import functools

import jax
import jax.numpy as jnp
from jax import lax
from jax.experimental import pallas as pl
from jax.experimental.pallas import tpu as pltpu
from jax.sharding import PartitionSpec as P

MESH = pl.DeviceIdType.MESH
YG = 64
CG = 6
SIGMA = 1e-06
RELAX = 1.6
B = 128
TPG = 16
F32 = jnp.float32
BF16 = jnp.bfloat16


def ring_distance(step, size):
    return min(step, size - step)


def peer_offsets(dims, weights):
    offsets = [()]
    for size in dims:
        offsets = [o + (s,) for o in offsets for s in range(size)]
    cost = lambda o: sum(w * ring_distance(s, n) for s, n, w in zip(o, dims, weights))
    return sorted([o for o in offsets if any(o)], key=cost, reverse=True)


def shifted(index, offset, dims, sign):
    out, stride = 0, 1
    for size, step in reversed(list(zip(dims, offset))):
        coord = lax.rem(lax.div(index, jnp.int32(stride)), jnp.int32(size))
        move = step if sign > 0 else (size - step) % size
        coord = lax.rem(coord + jnp.int32(move), jnp.int32(size))
        out = out + coord * jnp.int32(stride)
        stride *= size
    return out


def halves(value):
    high = value.astype(BF16)
    return high, (value - high.astype(F32)).astype(BF16)


def dot(a, b):
    return lax.dot_general(a, b, (((1,), (0,)), ((), ())), preferred_element_type=F32)


class Exchange:
    def __init__(self, axis, targets, senders, sems):
        self.axis, self.targets, self.senders, self.sems = axis, targets, senders, sems

    def copy(self, k, src, dst, peer):
        return pltpu.make_async_remote_copy(
            src_ref=src,
            dst_ref=dst,
            send_sem=self.sems.at[0, k],
            recv_sem=self.sems.at[1, k],
            device_id={self.axis: peer},
            device_id_type=MESH,
        )

    def start(self, src_of, dst_of):
        for k, peer in enumerate(self.targets):
            self.copy(k, src_of(peer), dst_of(peer), peer).start()

    def wait_recv(self, dst_from):
        for k, sender in enumerate(self.senders):
            self.copy(k, dst_from(sender), dst_from(sender), sender).wait_recv()

    def wait_send(self, src_of):
        for k, peer in enumerate(self.targets):
            self.copy(k, src_of(peer), src_of(peer), peer).wait_send()


def kernel(cfg, ct, ft, crow, ccol, frow, fcol, diag_in, q_in, x0_in, lb, ub, z0, y0, rho_ref,
           pn_o, sl_o, du_o, res_o,
           raw, tiles, ohct, ohrt, lane_ids, part, sqpart,
           ufull, yfull, bfull, pfull, xfull, yp, yx, ystart, x0t, prec, dfull, qt, rsh, ssh, gamma_ref, alpha_ref,
           rcv_c, rcv_r, rcv_q, scal_c, scal_r, scal_m, scal_n,
           load_sems, sem_rc, sem_ac, sem_sc, sem_rr, sem_ar, sem_sr, sem_q, sem_aq, sem_m, sem_n):
    nr, nc, ga, gg, rdims, cdims, roffs, coffs, yb = cfg
    ng = ga + gg
    row = lax.axis_index("row")
    col = lax.axis_index("col")
    jr, ic = B // nr, B // nc
    xw = ufull.shape[1]
    rho = rho_ref[0, 0]
    row_targets = [shifted(row, off, rdims, 1) for off in roffs]
    row_senders = [shifted(row, off, rdims, -1) for off in roffs]
    col_targets = [shifted(col, off, cdims, 1) for off in coffs]
    col_senders = [shifted(col, off, cdims, -1) for off in coffs]

    barrier = pltpu.get_barrier_semaphore()
    for peer in row_targets:
        pl.semaphore_signal(barrier, inc=1, device_id={"row": peer}, device_id_type=MESH)
    for peer in col_targets:
        pl.semaphore_signal(barrier, inc=1, device_id={"col": peer}, device_id_type=MESH)

    def load(g):
        src = ct.at[pl.ds(g * TPG, TPG)] if g < ga else ft.at[pl.ds((g - ga) * TPG, TPG)]
        return pltpu.make_async_copy(src, raw.at[g], load_sems.at[g])

    for g in range(ng):
        load(g).start()

    def ex(axis, sems):
        if axis == "row":
            return Exchange("row", row_targets, row_senders, sems)
        return Exchange("col", col_targets, col_senders, sems)

    x_rc, x_ac, x_sc = ex("col", sem_rc), ex("col", sem_ac), ex("col", sem_sc)
    x_rr, x_ar, x_sr = ex("row", sem_rr), ex("row", sem_ar), ex("row", sem_sr)
    x_q, x_aq, x_m, x_n = ex("row", sem_q), ex("row", sem_aq), ex("row", sem_m), ex("col", sem_n)

    jrows = lambda i: pl.ds(pl.multiple_of(i * jr, jr), jr)
    irows = lambda i: pl.ds(pl.multiple_of(i * ic, ic), ic)
    mine_j, mine_i = jrows(row), irows(col)

    def transposed(ref, dst):
        for b in range(xw // B):
            dst[:, b * B:(b + 1) * B] = ref[b * B:(b + 1) * B, :].T

    transposed(x0_in, x0t)
    transposed(diag_in, dfull)
    transposed(q_in, qt)
    ufull[...] = x0t[...]
    xfull[...] = x0t[...]
    pfull[...] = jnp.zeros_like(pfull)
    yp[...] = jnp.zeros_like(yp)
    ssh[...] = jnp.zeros_like(ssh)
    scal_c[...] = jnp.zeros_like(scal_c)
    gamma_ref[...] = jnp.ones_like(gamma_ref)
    alpha_ref[...] = jnp.ones_like(alpha_ref)
    first = rho * z0[...] - y0[...]
    first = jnp.concatenate([first, jnp.zeros((xw - yb, B), F32)], axis=0)
    for b in range(xw // B):
        bfull[:, b * B:(b + 1) * B] = first[b * B:(b + 1) * B, :].T

    def spread(ref, groups):
        count = groups * TPG
        wide = jnp.broadcast_to(ref[...].astype(F32), (16, count))
        own = lax.broadcasted_iota(jnp.int32, (16, count), 1) // TPG == lax.broadcasted_iota(jnp.int32, (16, count), 0)
        pick = lax.rem(lax.broadcasted_iota(jnp.int32, (count, B), 0), jnp.int32(TPG)) == (
            lax.broadcasted_iota(jnp.int32, (count, B), 1) // 8)
        return dot(jnp.where(own, wide, 0.0).astype(BF16), jnp.where(pick, 1.0, 0.0).astype(BF16))

    lane_ids[0, 0:16, :] = spread(ccol, ga)
    lane_ids[0, 16:32, :] = spread(fcol, gg)
    lane_ids[1, 0:16, :] = spread(crow, ga)
    lane_ids[1, 16:32, :] = spread(frow, gg) + float(yb)
    slot = lambda g: g if g < ga else 16 + g - ga

    for which, oht in enumerate((ohct, ohrt)):
        for g in range(ng):
            ids = jnp.broadcast_to(lane_ids[which, slot(g):slot(g) + 1, :], (B, B)).T
            tall = jnp.concatenate([ids] * (xw // B), axis=1)
            blocks = lax.broadcasted_iota(jnp.int32, (B, xw), 1).astype(F32)
            hot = jnp.where(tall == blocks, 1.0, 0.0).astype(BF16)
            oht[g, 0:B, :] = hot
            oht[g, B:2 * B, :] = hot

    mask = jnp.where(
        lax.rem(lax.broadcasted_iota(jnp.int32, (8, B), 1), jnp.int32(8)) == lax.broadcasted_iota(jnp.int32, (8, B), 0),
        1.0, 0.0).astype(F32)

    def scattered(value, onehot_t):
        return dot(jnp.concatenate(halves(value), axis=1), onehot_t)

    def relayout(g, _):
        pltpu.make_async_copy(ct.at[pl.ds(0, TPG)], raw.at[g], load_sems.at[g]).wait()
        total = jnp.zeros((B, B), F32)
        for i in range(B // 8):
            block = raw[g, :, 8 * i:8 * i + 8, :].reshape(B, B).T
            tiles[g, i] = block
            total = total + block * block
        raw[g, 0] = total * jnp.where(g < ga, rho, 1.0)
        return 0

    lax.fori_loop(0, ng, relayout, 0)
    total = scattered(raw[0, 0], ohct[0])
    for g in range(1, ng):
        total = total + scattered(raw[g, 0], ohct[g])
    sqpart[...] = total

    def gathered(ref, which, g):
        ids = jnp.broadcast_to(lane_ids[which, slot(g):slot(g) + 1, :], (8, B)).astype(jnp.int32)
        within = lax.rem(ids, jnp.int32(B))
        out = []
        for i in range(B // 8):
            rows = slice(8 * i, 8 * i + 8)
            value = jnp.take_along_axis(ref[rows, 0:B], within, axis=1)
            for b in range(1, xw // B):
                other = jnp.take_along_axis(ref[rows, b * B:(b + 1) * B], within, axis=1)
                value = jnp.where(ids < b * B, value, other)
            out.append(value)
        return out

    def forward():
        total = None
        for g in range(ng):
            v = gathered(ufull, 0, g)
            rows = []
            for i in range(B // 8):
                prod = tiles[g, i, 0:8, :] * v[0]
                for j in range(1, B // 8):
                    prod = prod + tiles[g, i, 8 * j:8 * j + 8, :] * v[j]
                rows.append(prod.sum(axis=0, keepdims=True) * mask)
            share = scattered(jnp.concatenate(rows, axis=0), ohrt[g])
            total = share if total is None else total + share
        part[...] = total

    def backward():
        total = None
        for g in range(ng):
            us = [(v * mask).sum(axis=0, keepdims=True) for v in gathered(bfull, 1, g)]
            us = [jnp.broadcast_to(u, (8, B)) for u in us]
            rows = []
            for j in range(B // 8):
                acc = tiles[g, 0, 8 * j:8 * j + 8, :] * us[0]
                for i in range(1, B // 8):
                    acc = acc + tiles[g, i, 8 * j:8 * j + 8, :] * us[i]
                rows.append(acc)
            share = scattered(jnp.concatenate(rows, axis=0), ohct[g])
            total = share if total is None else total + share
        part[...] = total

    lane_x = lax.broadcasted_iota(jnp.int32, (1, xw), 1)
    weight = jnp.where(lane_x < yb, rho, 1.0)

    def fold(value):
        s = value.sum(axis=0, keepdims=True)
        out = s[:, :B]
        for b in range(1, xw // B):
            out = out + s[:, b * B:(b + 1) * B]
        return out

    def fold_max(value):
        s = value.max(axis=0, keepdims=True)
        out = s[:, :B]
        for b in range(1, xw // B):
            out = jnp.maximum(out, s[:, b * B:(b + 1) * B])
        return out

    part_i, part_j = (lambda p: part.at[irows(p)]), (lambda p: part.at[jrows(p)])
    sq_j = lambda p: sqpart.at[jrows(p)]
    y_mine, u_mine, prec_mine = (lambda p: yfull.at[mine_i]), (lambda p: ufull.at[mine_j]), (lambda p: prec.at[mine_j])
    sc_mine, sr_mine = (lambda p: scal_c.at[col]), (lambda p: scal_r.at[row])

    def finish_rr():
        x_rr.wait_recv(lambda s: rcv_r.at[s])
        total = part[mine_j, :]
        for sender in row_senders:
            total = total + rcv_r[sender]
        return total

    def step_length(gamma_new, dx, beta):
        x_sr.wait_recv(lambda s: scal_r.at[s])
        delta = dx + scal_r[...].sum(axis=0).sum(axis=1, keepdims=True)
        alpha = gamma_new / (delta - beta * gamma_new / alpha_ref[...])
        alpha_ref[...] = alpha
        x_sr.wait_send(sr_mine)
        return alpha

    def follow(alpha, beta):
        xfull[...] = xfull[...] + alpha * pfull[...]
        y = yfull[...] + beta * yp[...]
        yp[...] = y
        yx[...] = yx[...] + alpha * y

    pl.semaphore_wait(barrier, len(roffs) + len(coffs))
    x_q.start(sq_j, lambda p: rcv_q.at[row])

    last = CG

    def step(t, _):
        @pl.when(t > 0)
        def _():
            u = ufull[...]
            square = u * u
            scal_c[col, 0:1, :] = fold(prec[...] * square)
            scal_c[col, 1:2, :] = fold((dfull[...] + SIGMA) * square)
            x_sc.start(sc_mine, sc_mine)

        forward()
        x_rc.start(part_i, lambda p: rcv_c.at[col])

        @pl.when(t == 0)
        def _():
            x_q.wait_recv(lambda s: rcv_q.at[s])
            total = sqpart[mine_j, :] + dfull[mine_j, :] + SIGMA
            for sender in row_senders:
                total = total + rcv_q[sender]
            prec[mine_j, :] = total
            x_aq.start(prec_mine, prec_mine)
            x_q.wait_send(sq_j)

        @pl.when(t > 0)
        def _():
            x_sc.wait_recv(lambda s: scal_c.at[s])
            x_sc.wait_send(sc_mine)

        sums = scal_c[...].sum(axis=0)
        sums = sums.sum(axis=1, keepdims=True)
        gamma_new, dx = sums[0:1, :], sums[1:2, :]
        beta = jnp.where(t > 1, gamma_new / gamma_ref[...], 0.0)
        gamma_ref[...] = gamma_new

        x_rc.wait_recv(lambda s: rcv_c.at[s])
        total = part[mine_i, :]
        for sender in col_senders:
            total = total + rcv_c[sender]
        yfull[mine_i, :] = total
        x_ac.start(y_mine, y_mine)
        x_rc.wait_send(part_i)
        pfull[...] = ufull[...] + beta * pfull[...]
        x_ac.wait_recv(lambda s: yfull.at[irows(s)])

        @pl.when(t == 0)
        def _():
            y = yfull[...]
            ystart[...] = y
            yx[...] = y
            bfull[...] = bfull[...] - weight * y

        @pl.when(t > 0)
        def _():
            y = yfull[...]
            wy = weight * y
            bfull[...] = wy
            scal_r[row] = fold(wy * y)
            x_sr.start(sr_mine, sr_mine)

        @pl.when(t == last)
        def _():
            follow(step_length(gamma_new, dx, beta), beta)
            for b in range(xw // B):
                at = slice(b * B, (b + 1) * B)
                rows = min(yb - b * B, B)
                rs = slice(b * B, b * B + rows)
                yx_t = yx[:, at].T
                relaxed = RELAX * yx_t[:rows] + (1.0 - RELAX) * z0[rs, :]
                dual = y0[rs, :]
                slack = jnp.minimum(jnp.maximum(relaxed + dual / rho, lb[rs, :]), ub[rs, :])
                dual = dual + rho * (relaxed - slack)
                sl_o[rs, :] = slack
                du_o[rs, :] = dual
                image = RELAX * yx_t + (1.0 - RELAX) * ystart[:, at].T
                gap = jnp.abs(image[:rows] - slack).max(axis=0, keepdims=True)
                primal = gap if b == 0 else jnp.maximum(primal, gap)
                if rows < B:
                    dual = jnp.concatenate([dual, image[rows:]], axis=0)
                bfull[:, at] = dual.T
            scal_m[row, 0:1, :] = primal

        x_ac.wait_send(y_mine)
        backward()
        x_rr.start(part_j, lambda p: rcv_r.at[row])

        @pl.when(t == 0)
        def _():
            x_aq.wait_recv(lambda s: prec.at[jrows(s)])
            x_aq.wait_send(prec_mine)
            resid = finish_rr() - qt[mine_j, :] - dfull[mine_j, :] * x0t[mine_j, :]
            rsh[...] = resid
            ufull[mine_j, :] = resid / prec[mine_j, :]

        @pl.when(jnp.logical_and(t > 0, t < last))
        def _():
            alpha = step_length(gamma_new, dx, beta)
            image = (dfull[mine_j, :] + SIGMA) * ufull[mine_j, :] + beta * ssh[...]
            along = finish_rr() + image
            ssh[...] = along
            resid = rsh[...] - alpha * along
            rsh[...] = resid
            ufull[mine_j, :] = resid / prec[mine_j, :]

        @pl.when(t < last)
        def _():
            x_ar.start(u_mine, u_mine)
            x_rr.wait_send(part_j)

            @pl.when(t > 0)
            def _():
                follow(alpha_ref[...], beta)

            x_ar.wait_recv(lambda s: ufull.at[jrows(s)])
            x_ar.wait_send(u_mine)

        return 0

    lax.fori_loop(0, last + 1, step, 0)
    pfull[...] = RELAX * xfull[...] + (1.0 - RELAX) * x0t[...]
    for b in range(xw // B):
        pn_o[b * B:(b + 1) * B, :] = pfull[:, b * B:(b + 1) * B].T
    known = dfull[mine_j, :] * pfull[mine_j, :] + qt[mine_j, :]
    dvec = finish_rr() + known
    scal_m[row, 1:2, :] = fold_max(jnp.abs(dvec))
    sm_mine, sn_mine = (lambda p: scal_m.at[row]), (lambda p: scal_n.at[col])
    x_m.start(sm_mine, sm_mine)
    x_rr.wait_send(part_j)
    x_m.wait_recv(lambda s: scal_m.at[s])
    scal_n[col] = scal_m[...].max(axis=0)
    x_n.start(sn_mine, sn_mine)
    x_m.wait_send(sm_mine)
    x_n.wait_recv(lambda s: scal_n.at[s])
    x_n.wait_send(sn_mine)
    worst = scal_n[...].max(axis=0).max(axis=1, keepdims=True)
    res_o[...] = jnp.broadcast_to(worst, res_o.shape)


def hand_over(pn, sl, du, res, pn_o, sl_o, du_o, primal_o, dual_o):
    pn_o[...] = pn[...]
    sl_o[...] = sl[...]
    du_o[...] = du[...]
    primal_o[...] = res[0:1, 0:1]
    dual_o[...] = res[1:2, 0:1]


def local(dims, ct, crow, ccol, ft, frow, fcol, diag, q, lb, ub, x0, z0, y0, penalty):
    nr, nc, rdims, cdims, rweights, cweights = dims
    ka, kg = ct.shape[0], ft.shape[0]
    ct, ft = ct.reshape(ka, B, B), ft.reshape(kg, B, B)
    ga, gg = ka // TPG, kg // TPG
    ng = ga + gg
    yb = z0.shape[0]
    xw = x0.shape[0]
    roffs = peer_offsets(rdims, rweights)
    coffs = peer_offsets(cdims, cweights)
    cfg = (nr, nc, ga, gg, rdims, cdims, roffs, coffs, yb)
    jr, ic = B // nr, B // nc
    vmem = pl.BlockSpec(memory_space=pltpu.VMEM)
    hbm = pl.BlockSpec(memory_space=pl.ANY)
    full = pltpu.VMEM((B, xw), F32)
    dma = pltpu.SemaphoreType.DMA
    csem, rsem = dma((2, len(coffs))), dma((2, len(roffs)))
    shapes = [jax.ShapeDtypeStruct(s, F32) for s in ((xw, B), (yb, B), (yb, B), (2, B))]
    outs = pl.pallas_call(
        functools.partial(kernel, cfg),
        out_shape=shapes,
        in_specs=[hbm, hbm] + [vmem] * 11 + [pl.BlockSpec(memory_space=pltpu.SMEM)],
        out_specs=[vmem] * 4,
        scratch_shapes=[
            pltpu.VMEM((ng, TPG, B, B), F32),
            pltpu.VMEM((ng, B // 8, B, B), F32),
            pltpu.VMEM((ng, 2 * B, xw), BF16),
            pltpu.VMEM((ng, 2 * B, xw), BF16),
            pltpu.VMEM((2, 32, B), F32),
            full, full,
            full, full, full, full, full, full, full, full, full, full, full, full,
            pltpu.VMEM((jr, xw), F32),
            pltpu.VMEM((jr, xw), F32),
            pltpu.VMEM((1, 1), F32),
            pltpu.VMEM((1, 1), F32),
            pltpu.VMEM((nc, ic, xw), F32),
            pltpu.VMEM((nr, jr, xw), F32),
            pltpu.VMEM((nr, jr, xw), F32),
            pltpu.VMEM((nc, 2, B), F32),
            pltpu.VMEM((nr, 1, B), F32),
            pltpu.VMEM((nr, 2, B), F32),
            pltpu.VMEM((nc, 2, B), F32),
            dma((ng,)),
            csem, csem, csem, rsem, rsem, rsem, rsem, rsem, rsem, csem,
        ],
        compiler_params=pltpu.CompilerParams(collective_id=0, has_side_effects=True),
    )(ct, ft, crow.reshape(1, ka), ccol.reshape(1, ka), frow.reshape(1, kg), fcol.reshape(1, kg),
      diag, q, x0, lb, ub, z0, y0, penalty.reshape(1, 1))
    one = jax.ShapeDtypeStruct((1, 1), F32)
    pn, sl, du, primal, dual = pl.pallas_call(
        hand_over,
        out_shape=shapes[:3] + [one, one],
        in_specs=[vmem] * 4,
        out_specs=[vmem] * 5,
    )(*outs)
    return pn, sl, du, primal[0, 0], dual[0, 0]


def solution(mesh):
    nr, nc = mesh.shape["row"], mesh.shape["col"]
    rdims, rweights = ((2, 4, 2), (2, 1, 0)) if nr == 16 else ((nr,), (1,))
    cdims, cweights = ((4, 2), (1, 1)) if nc == 8 else ((nc,), (1,))
    dims = (nr, nc, rdims, cdims, rweights, cweights)
    rc = P("row", "col")
    tiles = P("row", "col", None, None)
    xs, ys = P("col", None), P("row", None)
    return jax.shard_map(
        functools.partial(local, dims),
        mesh=mesh,
        in_specs=(tiles, rc, rc, tiles, rc, rc, xs, xs, ys, ys, xs, ys, ys, P()),
        out_specs=(xs, ys, ys, P(), P()),
        check_vma=False,
    )
```

time: 184 us -> 167 us (0.908)
  Pallas kernels: 174 us -> 166 us
  local copies, waits for them, and re-layouts: 6.69 us -> 0 us
  other arithmetic: 2.14 us -> 0 us
    pallas_call x1 -> x2, Pallas kernels: 174 us -> 166 us  [the longest x1 164 us: local(): pl.pallas_call(functools.partial(kernel, cfg), out_shape=shapes, in_specs...]
    unnamed x3 -> x0, local copies, waits for them, and re-layouts: 4.64 us -> none
where the time goes in v2:
time: 167 us
  Pallas kernels  166 us (99%)
    pallas_call x1, Pallas kernels, local(): pl.pallas_call(functools.partial(kernel, cfg), out_shape=shapes, in_specs...  164 us

profile of v2, /device:TPU:1, one launch (start us, length us, event | category | flops | bytes accessed | tf_op | source)
XLA Modules:
  0.0 166.9 jit_solution(12800824389303906559)
XLA Ops:
  1.3 163.9 %shard_map.173 = (f32[256,128]{1,0:T(8,128)}, f32[192,128]{1,0:T(8,128)}, f32[192,128]{1,0:T(8,128)}, f32[2,128]{1,0:T(2,128)}) custom-call(f32[96,128,128]{2,1,0:T(8,128)} %bitcast.10, f32[48,128,128]{2,1,0:T(8,128)} %bitcast.11, s32[1,96]{1,0:T(1,128)} %bitcast.12, s32[1,96]{1,0:T(1,128)} %bitcast.13, s32[1,48]{1,0:T(1,128)} %bitcast.14, ...), custom_call_target="tpu_custom_call" | custom-call | tf_op jit(solution)/shard_map/pallas_call | solution.py:442
  165.2 1.7 %shard_map.174 = (f32[256,128]{1,0:T(8,128)}, f32[192,128]{1,0:T(8,128)}, f32[192,128]{1,0:T(8,128)}, f32[1,1]{1,0:T(1,128)}, f32[1,1]{1,0:T(1,128)}) custom-call(f32[256,128]{1,0:T(8,128)} %get-tuple-element.14.pn, f32[192,128]{1,0:T(8,128)} %get-tuple-element.15.sl, f32[192,128]{1,0:T(8,128)} %get-tuple-element.16.du, f32[2,128]{1,0:T(2,128)} %get-tuple-element.17.res), custom_call_target="tpu_custom_call" | custom-call | tf_op jit(solution)/shard_map/pallas_call | solution.py:473
